TPU v7x, 32 devices: a whole 2x2x4 slice. The times are simulated.
32 devices in a mesh: ep: 8 (over z, x), corner: 4 (over y, core).
Axes of the slice: x: 2, y: 2, z: 4, core: 2. Of those that a mesh axis runs over, the one named last changes fastest.
Arguments:
- required: float32 [8, 262144], P('corner', 'ep'), may hold values from -3 to 3
- arrival: float32 [8, 262144], P('corner', 'ep'), may hold values from -7.2 to 7.2
- hold_required: float32 [8, 262144], P('corner', 'ep'), may hold values from -5.4 to 5.4
- early_arrival: float32 [8, 262144], P('corner', 'ep'), may hold values from -3 to 3
- part_ids: int32 [262144], P('ep'), may hold values from 0 to 63
- bin_edges: int32 [512], replicated, may hold values from -4096 to -1, as said below
Outputs:
- part_hist: float32 [64, 8, 2, 512], P(None, 'corner')
- part_tns: float32 [64, 8, 2], P(None, 'corner')
- part_share: float32 [64], replicated
- tns: float32 [8, 2], P('corner')
- wns: float32 [8, 2], P('corner')
- worst: float32 [2, 262144], P(None, 'ep')
Inputs may be any that keep to these rules, and one draw needn't show every extreme that they name: `bin_edges`: strictly increasing and negative; consecutive nodes differ by 1 to 8.
All inputs are finite; a program needn't handle non-finite values.
Results may differ from a plain program's by a relative error of at most 0.0003.
Values sent between devices are 32-bit elements; how exact they have to be, the bound alone decides.
No kernel may reach another device: no remote copies, remote signals or barrier semaphores. Data moves between devices by JAX's collectives and lax.ppermute only.
A program may use at most 64 MiB of HBM per device.

v0:
```python
import functools
import jax
import jax.numpy as jnp
from jax import lax
from jax.experimental import pallas as pl
from jax.experimental.pallas import tpu as pltpu
from jax.sharding import PartitionSpec as P

GROUPS = 64
LANES = 128
LEAST = 4096
F8 = jnp.float8_e4m3fn
BF = jnp.bfloat16
STEP = 0.001
VMEM = 12 << 20
EXTRA = 8


def lookup(table_ref, index):
    lane = index & (LANES - 1)
    row = index >> 7
    out = None
    for r in range(table_ref.shape[0]):
        line = jnp.broadcast_to(table_ref[r:r + 1, :], index.shape)
        got = jnp.take_along_axis(line, lane, axis=1, mode="promise_in_bounds")
        out = got if out is None else jnp.where(row == r, got, out)
    return out


def interval(slack, x0, coarse_ref, fine_ref):
    t = jnp.minimum(jnp.maximum(slack, x0), 0.0)
    whole = jnp.floor(t * 1000.0)
    whole = jnp.where(t >= (whole + 1.0) * jnp.float32(STEP), whole + 1.0, whole)
    whole = jnp.where(t < whole * jnp.float32(STEP), whole - 1.0, whole)
    q = jnp.minimum(whole.astype(jnp.int32) + LEAST, LEAST - 1)
    cell = lookup(coarse_ref, q >> 3)
    upto = jnp.left_shift(2, q & 7) - 1
    j = (cell & 0xFFFF) + lax.population_count((cell >> 16) & upto) - 1
    pair = lookup(fine_ref, j)
    k = (pair & 0xFFFF) - LEAST
    x = k.astype(jnp.float32) * jnp.float32(STEP)
    xn = (k + (pair >> 16)).astype(jnp.float32) * jnp.float32(STEP)
    r = 1.0 / (xn - x)
    w1 = jnp.maximum((xn - t) * r, 0.0)
    w2 = jnp.maximum((t - x) * r, 0.0)
    local = j & (LANES - 1)
    odd = (j & 1) == 1
    even_place = ((local + 1) & ~1).astype(jnp.float32)
    odd_place = (local | 1).astype(jnp.float32)
    return (
        even_place,
        odd_place,
        jnp.where(odd, w2, w1),
        jnp.where(odd, w1, w2),
        (j >> 7).astype(jnp.float32),
        jnp.minimum(slack, 0.0),
    )


def prep_kernel(C, side_ref, *refs):
    sources, refs = refs[:6], refs[6:]
    (coarse_ref, fine_ref, worst_ref, keep_ref, send_ref), held, sems = refs[:5], refs[5:11], refs[11]
    copies = [pltpu.make_async_copy(src, dst, sems.at[i]) for i, (src, dst) in enumerate(zip(sources, held))]
    for copy in copies:
        copy.start()
    lines_ref, ids_ref, a_ref, b_ref, c_ref, d_ref = held
    copies[0].wait()
    lane = lax.broadcasted_iota(jnp.int32, (8, LANES), 1)
    counts = [jnp.zeros((8, LANES), jnp.int32) for _ in range(coarse_ref.shape[0])]
    for r in range(lines_ref.shape[0]):
        nodes = jnp.broadcast_to(lines_ref[r:r + 1, :] + LEAST, (LANES, LANES)).T
        for g in range(LANES // 8):
            node = nodes[g * 8:g * 8 + 8]
            here, bit = node >> 3, jnp.left_shift(65536, node & 7)
            for i in range(len(counts)):
                cell = lane + i * LANES
                counts[i] = counts[i] + jnp.where(here < cell, 1, jnp.where(here == cell, bit, 0))
    for i, count in enumerate(counts):
        coarse_ref[i:i + 1, :] = jnp.sum(count, axis=0, keepdims=True)
    q = lines_ref[...] + LEAST
    _, lanes = q.shape
    left = pltpu.roll(q, lanes - 1, 1)
    below = jnp.concatenate([left[1:], jnp.full((1, lanes), LEAST, jnp.int32)], axis=0)
    last = lax.broadcasted_iota(jnp.int32, q.shape, 1) == lanes - 1
    following = jnp.where(last, below, left)
    fine_ref[...] = q + (following - q) * 65536

    for copy in copies[1:]:
        copy.wait()
    flag = side_ref[0] == 0
    half = C // 2
    lines = a_ref.shape[0] // C
    for m, (late, early) in enumerate(((a_ref, b_ref), (c_ref, d_ref))):
        for k in range(half):
            pieces = []
            for c in (k, k + half):
                at = pl.ds(c, lines, stride=C)
                pieces.append(late[at, :] - early[at, :])
            keep_ref[m, pl.ds(k, lines, stride=half), :] = jnp.where(flag, pieces[0], pieces[1])
            send_ref[m, pl.ds(k, lines, stride=half), :] = jnp.where(flag, pieces[1], pieces[0])
            for piece in pieces:
                first = k == 0 and piece is pieces[0]
                at = pl.ds(m, lines, stride=2)
                worst_ref[at, :] = piece if first else jnp.minimum(worst_ref[at, :], piece)
    ids = ids_ref[...].astype(jnp.float32)
    keep_ref[2, :lines, :] = ids
    send_ref[2, :lines, :] = ids


def run_prep(edges, side, ids, a, b, c, d, C):
    bins = edges.shape[0]
    lines = ids.shape[0]
    sources = (edges.reshape(-1, LANES), ids, a, b, c, d)
    sources = [pltpu.with_memory_space_constraint(x, pltpu.HBM) for x in sources]
    held = [pltpu.VMEM(x.shape, x.dtype) for x in sources]
    return pl.pallas_call(
        functools.partial(prep_kernel, C),
        in_specs=[pl.BlockSpec(memory_space=pltpu.SMEM)] + [pl.BlockSpec(memory_space=pltpu.HBM)] * 6,
        out_shape=[
            jax.ShapeDtypeStruct((LEAST // 8 // LANES, LANES), jnp.int32),
            jax.ShapeDtypeStruct((bins // LANES, LANES), jnp.int32),
            jax.ShapeDtypeStruct((2 * lines, LANES), jnp.float32),
            jax.ShapeDtypeStruct((3, lines * C // 2, LANES), jnp.float32),
            jax.ShapeDtypeStruct((3, lines * C // 2, LANES), jnp.float32),
        ],
        scratch_shapes=held + [pltpu.SemaphoreType.DMA((6,))],
        compiler_params=pltpu.CompilerParams(vmem_limit_bytes=VMEM),
        name="prep",
    )(side, *sources)


def hist_kernel(C, KT, n, place_ref, coarse_ref, fine_ref, slack_ref, *refs):
    if n:
        prior_ref, prior_low_ref = refs[:2]
        outs, (low_ref, buf0, buf1, zed0, zed1, all_ref) = refs[2:2 + n], refs[2 + n:]
    else:
        out_ref, low_ref, buf0, buf1, zed0, zed1 = refs
    series = 2 * C
    nblk = fine_ref.shape[0]
    lines = KT * C
    chunks = slack_ref.shape[1] // lines
    x0 = ((fine_ref[:1, :1] & 0xFFFF) - LEAST).astype(jnp.float32) * jnp.float32(STEP)

    def body(*refs):
        for a in refs:
            pltpu.matmul_pop(a)
        accs, zaccs = refs[:series], refs[series:]
        iota16 = lax.broadcasted_iota(jnp.int32, (16, LANES), 0)
        iotas = [(iota16 + 16 * v).astype(jnp.float32).astype(BF) for v in range(LANES // 16)]
        iota32 = lax.broadcasted_iota(jnp.int32, (32, LANES), 0)
        iotas32 = [(iota32 + 32 * v).astype(jnp.float32).astype(BF) for v in range(GROUPS // 32)]
        even = (iota16 & 1) == 0
        iota8 = lax.broadcasted_iota(jnp.int32, (8, LANES), 0)
        one = jnp.ones((32, LANES), jnp.float32).astype(F8)
        zero16 = jnp.zeros((16, LANES), BF)
        none = jnp.zeros((32, LANES), F8)
        blank = jnp.where(iota8 == 3, 1.0, 0.0)

        def wide(x, rows):
            return jnp.broadcast_to(x, (rows, LANES))

        def look(buf, zed, chunk, g):
            start = pl.multiple_of(chunk * lines + g * 8, 8)
            at = pl.ds(start, 8)
            for m in range(2):
                slack = slack_ref[m, at, :]
                low_ref[m] = jnp.minimum(low_ref[m], slack)
                found = interval(slack, x0, coarse_ref, fine_ref)
                for i, v in enumerate(found[:5]):
                    buf[i, m, g * 8:g * 8 + 8, :] = v
                high = found[5].astype(BF).astype(jnp.float32)
                cross = jnp.where(found[0] == float(LANES), found[2], 0.0)
                parts = {0: high, 1: found[5] - high}
                for h in range(nblk - 1):
                    parts[4 + h] = jnp.where(found[4] == float(h), cross, 0.0)
                for i, v in parts.items():
                    zed[m, pl.ds(g * 64 + i, 8, stride=8), :] = v

        def pair(buf, zed, chunk, k2):
            member = []
            for kk in range(2):
                ids = wide(slack_ref[2, pl.ds(chunk * KT + 2 * k2 + kk, 1), :], 32).astype(BF)
                member.append([jnp.where(i == ids, one, none) for i in iotas32])
            for s in range(series):
                c, m = divmod(s, 2)
                left, right = [], []
                for kk in range(2):
                    r = (2 * k2 + kk) * C + c
                    row = [buf[i, m, r:r + 1, :] for i in range(5)]
                    block = wide(row[4], 32).astype(BF)
                    left.append(jnp.concatenate([
                        jnp.where(block == jnp.bfloat16(h), part, none) for h in range(nblk) for part in member[kk]
                    ], axis=0))
                    place = jnp.where(even, wide(row[0], 16), wide(row[1], 16)).astype(BF)
                    weight = jnp.where(even, wide(row[2], 16), wide(row[3], 16)).astype(BF)
                    hats = [jnp.where(i == place, weight, zero16) for i in iotas]
                    right.append(jnp.concatenate(hats, axis=0))
                pltpu.matmul_push_rhs(
                    jnp.concatenate(left, axis=1), staging_register=0, mxu_index=s % 2, transpose=True
                )
                pltpu.matmul_acc_lhs(accs[s], jnp.concatenate(right, axis=1), load_staged_rhs=0)
                if m == k2 % 2:
                    extra = []
                    for kk in range(2):
                        r = (2 * k2 + kk) * C + c
                        both_kinds = [zed[i, r * 8:r * 8 + 8, :] for i in (m, 1 - m)]
                        extra.append(jnp.concatenate(both_kinds, axis=0).astype(BF))
                    pltpu.matmul_acc_lhs(zaccs[s], jnp.concatenate(extra, axis=1))

        def both(chunk, buf, zed, ahead, other, other_zed):
            pairs, groups = KT // 2, lines // 8
            done = 0
            for k2 in range(pairs):
                pair(buf, zed, chunk, k2)
                while done < groups and done * pairs <= k2 * groups:
                    look(other, other_zed, ahead, done)
                    done += 1

        low_ref[...] = prior_low_ref[...] if n else jnp.full(low_ref.shape, jnp.inf)
        for zed in (zed0, zed1):
            for m in range(2):
                for r in range(lines):
                    zed[m, r * 8:r * 8 + 8, :] = blank
        for g in range(lines // 8):
            look(buf0, zed0, 0, g)

        def two(i, carry):
            both(2 * i, buf0, zed0, 2 * i + 1, buf1, zed1)
            both(2 * i + 1, buf1, zed1, jnp.minimum(2 * i + 2, chunks - 1), buf0, zed0)
            return carry

        lax.fori_loop(0, chunks // 2, two, 0)

        sums = [pltpu.matmul_pop(a) for a in accs]
        zeds = [pltpu.matmul_pop(a) for a in zaccs]
        if not n:
            for s in range(series):
                out_ref[s, :LANES] = sums[s]
                out_ref[s, LANES:] = zeds[s]
            return
        zeds = [prior_ref[s, LANES:] + zeds[s] for s in range(series)]
        own = GROUPS // n
        lane = lax.broadcasted_iota(jnp.int32, (8, LANES), 1)
        sub = lax.broadcasted_iota(jnp.int32, (8, LANES), 0)
        wide_lane = lax.broadcasted_iota(jnp.int32, (8, nblk * GROUPS), 1)
        wide_sub = lax.broadcasted_iota(jnp.int32, (8, nblk * GROUPS), 0)
        chunk_rows = outs[0].shape[0]
        hist_rows = own * series * nblk
        tile = jnp.zeros((8, LANES), jnp.float32)
        for s in range(series):
            c, m = divmod(s, 2)
            total = prior_ref[s, :LANES] + sums[s]
            stats = zeds[s][:8] + zeds[s ^ 1][8:]
            folded = stats[:, :LANES]
            for v in range(1, nblk * GROUPS // LANES):
                folded = folded + stats[:, v * LANES:(v + 1) * LANES]
            folded = folded + pltpu.roll(folded, GROUPS, 1)
            passed = jnp.where(lane < GROUPS, 0.0, folded[4:5])[:1]
            passed = [passed] + [
                jnp.where(lane < GROUPS, folded[2 * v + 3:2 * v + 4], folded[2 * v + 4:2 * v + 5])[:1]
                for v in range(1, nblk * GROUPS // LANES)
            ]
            across = jnp.broadcast_to(jnp.concatenate(passed, axis=1), wide_lane.shape)
            top = total[:8] + jnp.where((wide_sub == 0) & (wide_lane >= GROUPS), across, 0.0)
            full = jnp.concatenate([top, total[8:LANES]], axis=0).T
            low = jnp.min(jnp.where(sub % C == c, low_ref[m], jnp.inf), keepdims=True)
            row = jnp.where(lane < GROUPS, folded[0:1] + folded[1:2], low)
            tile = jnp.where(sub == s, row, tile)
            if s == 0:
                tile = jnp.where(sub == series, folded[3:4], tile)
            for h in range(nblk):
                for i in range(n):
                    at = i * chunk_rows + (c * nblk + h) * 2 + m
                    first = h * GROUPS + i * own
                    all_ref[pl.ds(at, own, stride=series * nblk), :] = full[first:first + own]
        for i in range(n):
            at = i * chunk_rows + hist_rows
            all_ref[at:at + EXTRA, :] = tile
        for d in range(n):
            at = pl.multiple_of((place_ref[0] ^ d) * chunk_rows, 8)
            outs[d][...] = all_ref[pl.ds(at, chunk_rows), :]

    shapes = [(LANES, nblk * GROUPS)] * series + [(16, nblk * GROUPS)] * series
    pl.run_scoped(body, *[pltpu.ACC(i % 2)(shape, jnp.float32) for i, shape in enumerate(shapes)])


def run_hist(place, coarse, fine, slack, C, n=0, prior=(), KT=32):
    nblk = fine.shape[0]
    series = 2 * C
    smem = pl.BlockSpec(memory_space=pltpu.SMEM)
    vm = pl.BlockSpec(memory_space=pltpu.VMEM)
    scratch = [pltpu.VMEM((5, 2, KT * C, LANES), jnp.float32) for _ in range(2)]
    scratch += [pltpu.VMEM((2, KT * C * 8, LANES), jnp.float32) for _ in range(2)]
    low = jax.ShapeDtypeStruct((2, 8, LANES), jnp.float32)
    if n:
        own = GROUPS // n
        rows = own * series * nblk + EXTRA
        outs = [jax.ShapeDtypeStruct((rows, LANES), jnp.float32) for _ in range(n)]
        scratch += [pltpu.VMEM((2, 8, LANES), jnp.float32)] * 0 + [pltpu.VMEM((n * rows, LANES), jnp.float32)]
    else:
        outs = [jax.ShapeDtypeStruct((series, LANES + 16, nblk * GROUPS), jnp.float32)]
    return pl.pallas_call(
        functools.partial(hist_kernel, C, KT, n),
        in_specs=[smem] + [vm] * (3 + len(prior)),
        out_shape=outs + [low],
        scratch_shapes=scratch,
        cost_estimate=pl.CostEstimate(
            flops=4 * (LANES + 16) * 256 * slack.size // 3, bytes_accessed=8 * slack.size, transcendentals=slack.size
        ),
        compiler_params=pltpu.CompilerParams(vmem_limit_bytes=VMEM),
        name="hist",
    )(place, coarse, fine, slack, *prior)


def final_kernel(C, own, share, scale, me_ref, *refs):
    n = len(refs) - 5
    pieces = refs[:n]
    hist_ref, part_ref, share_ref, tns_ref, wns_ref = refs[n:]
    half = C // 2
    each = hist_ref.shape[0] // GROUPS // 2
    for d in range(n):
        source = me_ref[0] ^ d
        place, side = source >> 1, source & 1
        for p in range(own):
            at = pl.multiple_of((place * own + p) * 2 * each + side * each, 8)
            hist_ref[pl.ds(at, each), :] = pieces[d][p * each:(p + 1) * each, :]
    tns = jnp.zeros((C, 2), jnp.float32)
    wns = jnp.zeros((C, 2), jnp.float32)
    row = lax.broadcasted_iota(jnp.int32, (C, 2), 0)
    col = lax.broadcasted_iota(jnp.int32, (C, 2), 1)
    mine, other = pieces[0][own * each:, :], pieces[1][own * each:, :]
    even = me_ref[0] % 2 == 0
    for side in range(2):
        tile = jnp.where(even, mine, other) if side == 0 else jnp.where(even, other, mine)
        for s in range(2 * half):
            c, m = divmod(s, 2)
            c += side * half
            sums = tile[s:s + 1, :GROUPS]
            part_ref[c, m:m + 1, :] = sums * share
            here = (row == c) & (col == m)
            tns = jnp.where(here, jnp.sum(sums, keepdims=True) * scale, tns)
            wns = jnp.where(here, tile[s:s + 1, GROUPS:GROUPS + 1], wns)
    share_ref[...] = mine[2 * half:2 * half + 1, :GROUPS] * share
    tns_ref[...] = tns
    wns_ref[...] = wns


def run_final(me, pieces, C, own, rows, endpoints):
    vm = pl.BlockSpec(memory_space=pltpu.VMEM)
    return pl.pallas_call(
        functools.partial(final_kernel, C, own, GROUPS / endpoints, 1.0 / endpoints),
        in_specs=[pl.BlockSpec(memory_space=pltpu.SMEM)] + [vm] * len(pieces),
        out_shape=[
            jax.ShapeDtypeStruct((GROUPS * rows, LANES), jnp.float32),
            jax.ShapeDtypeStruct((C, 2, GROUPS), jnp.float32),
            jax.ShapeDtypeStruct((1, GROUPS), jnp.float32),
            jax.ShapeDtypeStruct((C, 2), jnp.float32),
            jax.ShapeDtypeStruct((C, 2), jnp.float32),
        ],
        compiler_params=pltpu.CompilerParams(vmem_limit_bytes=VMEM),
        name="final",
    )(me, *pieces)


def rotate(value, axis, distance):
    size = lax.axis_size(axis)
    return lax.ppermute(value, axis, [(i, (i + distance) % size) for i in range(size)])


def turned(index, odd):
    return jnp.where(odd, (index & ~3) | ((index & 1) << 1) | ((index >> 1) & 1), index)


def moved(value, target):
    n, blocks = lax.axis_size("ep"), lax.axis_size("corner")

    def place(i, k):
        return (i & ~3 | (i & 1) << 1 | (i >> 1) & 1) if k % 2 else i

    pairs = [(place(i, k) * blocks + k, place(target(i), k) * blocks + k) for i in range(n) for k in range(blocks)]
    return lax.ppermute(value, ("ep", "corner"), pairs)


def tiles(x):
    c, e = x.shape
    return x.reshape(c, e // LANES, LANES).transpose(1, 0, 2).reshape(-1, LANES)


def on_device(required, arrival, hold_required, early_arrival, part_ids, bin_edges):
    C, rows = required.shape
    bins = bin_edges.shape[0]
    n = lax.axis_size("ep")
    me = turned(lax.axis_index("ep"), lax.axis_index("corner") % 2 == 1)
    endpoints = rows * n
    density = GROUPS * bins / endpoints
    half = C // 2
    side = me % 2
    place = me // 2
    rest = n // 2
    data = (tiles(required), tiles(arrival), tiles(early_arrival), tiles(hold_required))
    ids = part_ids.reshape(-1, LANES)
    lines = ids.shape[0]
    coarse, fine, near, keep, send = run_prep(bin_edges, side.reshape(1), ids, *data, C)
    got = moved(send, lambda i: i ^ 1)
    prior = run_hist(place.reshape(1), coarse, fine, keep, half)
    chunks = run_hist(place.reshape(1), coarse, fine, got, half, rest, prior)
    shares = [rotate(near, "corner", d) for d in range(1, lax.axis_size("corner"))]

    own = GROUPS // rest
    nblk = bins // LANES
    each = C * nblk
    hrows = own * each
    total = chunks[0]
    row = lax.broadcasted_iota(jnp.int32, total.shape, 0)
    lane = lax.broadcasted_iota(jnp.int32, total.shape, 1)
    least = (row >= hrows) & (row < hrows + 2 * half) & (lane >= GROUPS)
    order = sorted(range(1, rest), key=lambda d: (d != rest // 2, d))
    for d in order:
        piece = moved(chunks[d], lambda i: i ^ 2 * d)
        total = jnp.where(least, jnp.minimum(total, piece), total + piece)
    mine = jnp.where(row < hrows, total * density, total)
    pieces = [mine] + [None] * (n - 1)
    for d in range(1, rest):
        pieces[2 * d] = moved(mine, lambda i: i ^ 2 * d)
    pieces[1] = moved(mine, lambda i: i ^ 1)
    for d in range(1, rest):
        pieces[2 * d + 1] = moved(pieces[2 * d], lambda i: i ^ 1)
    worst = functools.reduce(jnp.minimum, shares, near)
    worst = worst.reshape(lines, 2, LANES)
    worst = worst.transpose(1, 0, 2).reshape(2, rows)
    full, part_tns, part_share, tns, wns = run_final(me.reshape(1), pieces, C, own, 2 * each, endpoints)
    part_hist = full.reshape(GROUPS, C, nblk, 2, LANES).transpose(0, 1, 3, 2, 4).reshape(GROUPS, C, 2, bins)
    part_tns = part_tns.transpose(2, 0, 1)
    part_share = part_share.reshape(GROUPS)
    return (part_hist, part_tns, part_share, tns, wns, worst)


def solution(mesh):
    in_specs = (
        P("corner", "ep"),
        P("corner", "ep"),
        P("corner", "ep"),
        P("corner", "ep"),
        P("ep"),
        P(),
    )
    out_specs = (
        P(None, "corner", None, None),
        P(None, "corner", None),
        P(),
        P("corner", None),
        P("corner", None),
        P(None, "ep"),
    )
    return jax.shard_map(
        on_device, mesh=mesh, in_specs=in_specs, out_specs=out_specs, check_vma=False
    )
```

profile of v0, /device:TPU:0, one launch (start us, length us, event | category | flops | bytes accessed | tf_op | source)
XLA Modules:
  0.0 44.3 jit_solution(16516829511791522464)
XLA Ops:
  0.7 1.5 %prep.1 = (s32[4,128]{1,0:T(4,128)S(1)}, s32[4,128]{1,0:T(4,128)S(1)}, f32[512,128]{1,0:T(8,128)S(1)}, f32[3,256,128]{2,1,0:T(8,128)S(1)}, f32[3,256,128]{2,1,0:T(8,128)S(1)}) custom-call(s32[1]{0:T(128)} %bitcast.2.side_ref, s32[4,128]{1,0:T(4,128)} %bitcast.43, s32[256,128]{1,0:T(8,128)} %bitcast.42, f32[512,128]{1,0:T(8,128)} %bitcast.38, ...), custom_call_target="tpu_custom_call" | custom-call | tf_op jit(solution)/shard_map/prep/pallas_call | solution.py:116
  2.1 2.5 %collective-permute-start.13 = (f32[512,128]{1,0:T(8,128)S(1)}, f32[512,128]{1,0:T(8,128)S(1)}, u32[]{:S(2)}, u32[]{:S(2)}) collective-permute-start(f32[512,128]{1,0:T(8,128)S(1)} %get-tuple-element.37), channel_id=1, source_target_pairs={{0,3},{1,0},{2,1},{3,2},{4,7},{5,4},{6,5},{7,6},{8,11},{9,8},{10,9... | collective-permute-start | bytes 786440 | tf_op jit(solution)/shard_map/ppermute | solution.py:367
  4.6 0.6 %collective-permute-start.12 = (f32[512,128]{1,0:T(8,128)S(1)}, f32[512,128]{1,0:T(8,128)S(1)}, u32[]{:S(2)}, u32[]{:S(2)}) collective-permute-start(f32[512,128]{1,0:T(8,128)S(1)} %get-tuple-element.37), channel_id=1, source_target_pairs={{0,2},{1,3},{2,0},{3,1},{4,6},{5,7},{6,4},{7,5},{8,10},{9,11},{10,... | collective-permute-start | bytes 786440 | tf_op jit(solution)/shard_map/ppermute | solution.py:367
  5.3 1.5 %collective-permute-start = (f32[3,256,128]{2,1,0:T(8,128)S(1)}, f32[3,256,128]{2,1,0:T(8,128)S(1)}, u32[]{:S(2)}, u32[]{:S(2)}) collective-permute-start(f32[3,256,128]{2,1,0:T(8,128)S(1)} %get-tuple-element.24), channel_id=1, source_target_pairs={{0,4},{1,9},{2,6},{3,11},{4,0},{9,1},{6,2},{11,3},{8,12},{5,13},{1... | collective-permute-start | bytes 1179656 | tf_op jit(solution)/shard_map/ppermute | solution.py:381
  6.8 5.4 %hist.2 = (f32[2,144,256]{2,1,0:T(8,128)S(1)}, f32[2,8,128]{2,1,0:T(8,128)S(1)}) custom-call(s32[1]{0:T(128)} %bitcast.1.place_ref, s32[4,128]{1,0:T(4,128)S(1)} %get-tuple-element.22.coarse_ref, s32[4,128]{1,0:T(4,128)S(1)} %get-tuple-element.23.fine_ref, f32[3,256,128]{2,1,0:T(8,128)S(1)} %get-tuple-element.25.slack_ref), custom_call_target="tpu_custom_call" | custom-call | flops 4831838208 | bytes 786432 | tf_op jit(solution)/shard_map/hist/pallas_call | solution.py:302
  12.2 0.9 %collective-permute-done.slack_ref = f32[3,256,128]{2,1,0:T(8,128)S(1)} collective-permute-done((f32[3,256,128]{2,1,0:T(8,128)S(1)}, f32[3,256,128]{2,1,0:T(8,128)S(1)}, u32[]{:S(2)}, u32[]{:S(2)}) %collective-permute-start) | collective-permute-done | bytes 393248 | tf_op jit(solution)/shard_map/ppermute | solution.py:381
  13.0 5.6 %hist.3 = (f32[136,128]{1,0:T(8,128)S(1)}, f32[136,128]{1,0:T(8,128)S(1)}, f32[136,128]{1,0:T(8,128)S(1)}, f32[136,128]{1,0:T(8,128)S(1)}, f32[2,8,128]{2,1,0:T(8,128)}) custom-call(s32[1]{0:T(128)} %bitcast.1.place_ref, s32[4,128]{1,0:T(4,128)S(1)} %get-tuple-element.22.coarse_ref, s32[4,128]{1,0:T(4,128)S(1)} %get-tuple-element.23.fine_ref, ...), custom_call_target="tpu_custom_call" | custom-call | flops 4831838208 | bytes 786432 | tf_op jit(solution)/shard_map/hist/pallas_call | solution.py:302
  18.7 3.7 %collective-permute-start.3 = (f32[136,128]{1,0:T(8,128)S(1)}, f32[136,128]{1,0:T(8,128)S(1)}, u32[]{:S(2)}, u32[]{:S(2)}) collective-permute-start(f32[136,128]{1,0:T(8,128)S(1)} %get-tuple-element.31), channel_id=1, source_target_pairs={{0,24},{1,21},{2,26},{3,23},{4,28},{9,29},{6,30},{11,31},{8,16},{5... | collective-permute-start | bytes 208904 | tf_op jit(solution)/shard_map/ppermute | solution.py:381
  22.4 0.0 collective-permute-start.2
  22.4 0.8 %collective-permute-start.1 = (f32[136,128]{1,0:T(8,128)S(1)}, f32[136,128]{1,0:T(8,128)S(1)}, u32[]{:S(2)}, u32[]{:S(2)}) collective-permute-start(f32[136,128]{1,0:T(8,128)S(1)} %get-tuple-element.29), channel_id=1, source_target_pairs={{0,16},{1,17},{2,18},{3,19},{4,20},{9,25},{6,22},{11,27},{8,24},{5... | collective-permute-start | bytes 208904 | tf_op jit(solution)/shard_map/ppermute | solution.py:381
  23.1 1.9 %collective-permute-done.3 = f32[136,128]{1,0:T(8,128)S(1)} collective-permute-done((f32[136,128]{1,0:T(8,128)S(1)}, f32[136,128]{1,0:T(8,128)S(1)}, u32[]{:S(2)}, u32[]{:S(2)}) %collective-permute-start.3) | collective-permute-done | bytes 69664 | tf_op jit(solution)/shard_map/ppermute | solution.py:381
  25.1 0.0 collective-permute-start.11
  25.1 1.7 %collective-permute-done.2 = f32[136,128]{1,0:T(8,128)S(1)} collective-permute-done((f32[136,128]{1,0:T(8,128)S(1)}, f32[136,128]{1,0:T(8,128)S(1)}, u32[]{:S(2)}, u32[]{:S(2)}) %collective-permute-start.2) | collective-permute-done | bytes 69664 | tf_op jit(solution)/shard_map/ppermute | solution.py:381
  26.8 1.0 %collective-permute-done.1 = f32[136,128]{1,0:T(8,128)S(1)} collective-permute-done((f32[136,128]{1,0:T(8,128)S(1)}, f32[136,128]{1,0:T(8,128)S(1)}, u32[]{:S(2)}, u32[]{:S(2)}) %collective-permute-start.1) | collective-permute-done | bytes 69664 | tf_op jit(solution)/shard_map/ppermute | solution.py:381
  27.8 0.1 multiply_select_fusion.refs_0_
  27.9 1.9 %collective-permute-start.5 = (f32[136,128]{1,0:T(8,128)S(1)}, f32[136,128]{1,0:T(8,128)S(1)}, u32[]{:S(2)}, u32[]{:S(2)}) collective-permute-start(f32[136,128]{1,0:T(8,128)S(1)} %multiply_select_fusion.refs_0_), channel_id=1, source_target_pairs={{0,8},{1,5},{2,10},{3,7},{4,12},{9,13},{6,14},{11,15},{8,0},{5,1},... | collective-permute-start | bytes 208904 | tf_op jit(solution)/shard_map/ppermute | solution.py:381
  29.8 2.5 %collective-permute-start.7 = (f32[136,128]{1,0:T(8,128)S(1)}, f32[136,128]{1,0:T(8,128)S(1)}, u32[]{:S(2)}, u32[]{:S(2)}) collective-permute-start(f32[136,128]{1,0:T(8,128)S(1)} %multiply_select_fusion.refs_0_), channel_id=1, source_target_pairs={{0,16},{1,17},{2,18},{3,19},{4,20},{9,25},{6,22},{11,27},{8,24},{5... | collective-permute-start | bytes 208904 | tf_op jit(solution)/shard_map/ppermute | solution.py:381
  32.2 0.0 collective-permute-done.13
  32.2 0.1 collective-permute-start.9
  32.4 0.0 collective-permute-done.12
  32.4 1.3 %collective-permute-start.4 = (f32[136,128]{1,0:T(8,128)S(1)}, f32[136,128]{1,0:T(8,128)S(1)}, u32[]{:S(2)}, u32[]{:S(2)}) collective-permute-start(f32[136,128]{1,0:T(8,128)S(1)} %multiply_select_fusion.refs_0_), channel_id=1, source_target_pairs={{0,4},{1,9},{2,6},{3,11},{4,0},{9,1},{6,2},{11,3},{8,12},{5,13},{1... | collective-permute-start | bytes 208904 | tf_op jit(solution)/shard_map/ppermute | solution.py:381
  33.7 0.0 collective-permute-done.5.refs_2_
  33.7 0.7 %collective-permute-start.6 = (f32[136,128]{1,0:T(8,128)S(1)}, f32[136,128]{1,0:T(8,128)S(1)}, u32[]{:S(2)}, u32[]{:S(2)}) collective-permute-start(f32[136,128]{1,0:T(8,128)S(1)} %collective-permute-done.5.refs_2_), channel_id=1, source_target_pairs={{0,4},{1,9},{2,6},{3,11},{4,0},{9,1},{6,2},{11,3},{8,12},{5,13},{1... | collective-permute-start | bytes 208904 | tf_op jit(solution)/shard_map/ppermute | solution.py:381
  34.4 3.1 %collective-permute-done.7.refs_4_ = f32[136,128]{1,0:T(8,128)S(1)} collective-permute-done((f32[136,128]{1,0:T(8,128)S(1)}, f32[136,128]{1,0:T(8,128)S(1)}, u32[]{:S(2)}, u32[]{:S(2)}) %collective-permute-start.7) | collective-permute-done | bytes 69664 | tf_op jit(solution)/shard_map/ppermute | solution.py:381
  37.5 0.8 %collective-permute-start.8 = (f32[136,128]{1,0:T(8,128)S(1)}, f32[136,128]{1,0:T(8,128)S(1)}, u32[]{:S(2)}, u32[]{:S(2)}) collective-permute-start(f32[136,128]{1,0:T(8,128)S(1)} %collective-permute-done.7.refs_4_), channel_id=1, source_target_pairs={{0,4},{1,9},{2,6},{3,11},{4,0},{9,1},{6,2},{11,3},{8,12},{5,13},{1... | collective-permute-start | bytes 208904 | tf_op jit(solution)/shard_map/ppermute | solution.py:381
  38.2 0.9 %collective-permute-done.9.refs_6_ = f32[136,128]{1,0:T(8,128)S(1)} collective-permute-done((f32[136,128]{1,0:T(8,128)S(1)}, f32[136,128]{1,0:T(8,128)S(1)}, u32[]{:S(2)}, u32[]{:S(2)}) %collective-permute-start.9) | collective-permute-done | bytes 69664 | tf_op jit(solution)/shard_map/ppermute | solution.py:381
  39.1 1.0 %collective-permute-start.10 = (f32[136,128]{1,0:T(8,128)S(1)}, f32[136,128]{1,0:T(8,128)S(1)}, u32[]{:S(2)}, u32[]{:S(2)}) collective-permute-start(f32[136,128]{1,0:T(8,128)S(1)} %collective-permute-done.9.refs_6_), channel_id=1, source_target_pairs={{0,4},{1,9},{2,6},{3,11},{4,0},{9,1},{6,2},{11,3},{8,12},{5,13},{1... | collective-permute-start | bytes 208904 | tf_op jit(solution)/shard_map/ppermute | solution.py:381
  40.0 0.0 collective-permute-done.11
  40.0 0.8 %minimum_minimum_fusion = f32[512,128]{1,0:T(8,128)} fusion(f32[512,128]{1,0:T(8,128)S(1)} %collective-permute-done.13, f32[512,128]{1,0:T(8,128)S(1)} %collective-permute-done.12, f32[512,128]{1,0:T(8,128)S(1)} %get-tuple-element.37, f32[512,128]{1,0:T(8,128)S(1)} %collective-permute-done.11), kind=kLoop, calls=%fused_computation | loop fusion | flops 196608 | bytes 1310720 | tf_op jit(solution)/shard_map/min | solution.py:428
  40.8 0.0 collective-permute-done.4.refs_1_
  40.8 0.0 collective-permute-done.6.refs_3_
  40.8 0.9 %collective-permute-done.8.refs_5_ = f32[136,128]{1,0:T(8,128)S(1)} collective-permute-done((f32[136,128]{1,0:T(8,128)S(1)}, f32[136,128]{1,0:T(8,128)S(1)}, u32[]{:S(2)}, u32[]{:S(2)}) %collective-permute-start.8) | collective-permute-done | bytes 69664 | tf_op jit(solution)/shard_map/ppermute | solution.py:381
  41.8 1.6 %collective-permute-done.10.refs_7_ = f32[136,128]{1,0:T(8,128)S(1)} collective-permute-done((f32[136,128]{1,0:T(8,128)S(1)}, f32[136,128]{1,0:T(8,128)S(1)}, u32[]{:S(2)}, u32[]{:S(2)}) %collective-permute-start.10) | collective-permute-done | bytes 69664 | tf_op jit(solution)/shard_map/ppermute | solution.py:381
  43.4 0.9 %final.1 = (f32[1024,128]{1,0:T(8,128)}, f32[2,2,64]{2,1,0:T(2,128)}, f32[1,64]{1,0:T(1,128)}, f32[2,2]{1,0:T(2,128)}, f32[2,2]{1,0:T(2,128)}) custom-call(s32[1]{0:T(128)} %bitcast.me_ref, f32[136,128]{1,0:T(8,128)S(1)} %multiply_select_fusion.refs_0_, f32[136,128]{1,0:T(8,128)S(1)} %collective-permute-done.4.refs_1_, ...), custom_call_target="tpu_custom_call" | custom-call | tf_op jit(solution)/shard_map/final/pallas_call | solution.py:350
  (2 shorter events, 0.0 us)
Async XLA Ops:
  2.1 30.1 %collective-permute-start.13 = (f32[512,128]{1,0:T(8,128)S(1)}, f32[512,128]{1,0:T(8,128)S(1)}, u32[]{:S(2)}, u32[]{:S(2)}) collective-permute-start(f32[512,128]{1,0:T(8,128)S(1)} %get-tuple-element.37), channel_id=1, source_target_pairs={{0,3},{1,0},{2,1},{3,2},{4,7},{5,4},{6,5},{7,6},{8,11},{9,8},{10,9... | collective-permute-start | bytes 786440 | tf_op jit(solution)/shard_map/ppermute | solution.py:367
  4.6 27.7 %collective-permute-start.12 = (f32[512,128]{1,0:T(8,128)S(1)}, f32[512,128]{1,0:T(8,128)S(1)}, u32[]{:S(2)}, u32[]{:S(2)}) collective-permute-start(f32[512,128]{1,0:T(8,128)S(1)} %get-tuple-element.37), channel_id=1, source_target_pairs={{0,2},{1,3},{2,0},{3,1},{4,6},{5,7},{6,4},{7,5},{8,10},{9,11},{10,... | collective-permute-start | bytes 786440 | tf_op jit(solution)/shard_map/ppermute | solution.py:367
  5.3 7.8 %collective-permute-start = (f32[3,256,128]{2,1,0:T(8,128)S(1)}, f32[3,256,128]{2,1,0:T(8,128)S(1)}, u32[]{:S(2)}, u32[]{:S(2)}) collective-permute-start(f32[3,256,128]{2,1,0:T(8,128)S(1)} %get-tuple-element.24), channel_id=1, source_target_pairs={{0,4},{1,9},{2,6},{3,11},{4,0},{9,1},{6,2},{11,3},{8,12},{5,13},{1... | collective-permute-start | bytes 1179656 | tf_op jit(solution)/shard_map/ppermute | solution.py:381
  18.7 6.4 %collective-permute-start.3 = (f32[136,128]{1,0:T(8,128)S(1)}, f32[136,128]{1,0:T(8,128)S(1)}, u32[]{:S(2)}, u32[]{:S(2)}) collective-permute-start(f32[136,128]{1,0:T(8,128)S(1)} %get-tuple-element.31), channel_id=1, source_target_pairs={{0,24},{1,21},{2,26},{3,23},{4,28},{9,29},{6,30},{11,31},{8,16},{5... | collective-permute-start | bytes 208904 | tf_op jit(solution)/shard_map/ppermute | solution.py:381
  22.4 4.5 %collective-permute-start.2 = (f32[136,128]{1,0:T(8,128)S(1)}, f32[136,128]{1,0:T(8,128)S(1)}, u32[]{:S(2)}, u32[]{:S(2)}) collective-permute-start(f32[136,128]{1,0:T(8,128)S(1)} %get-tuple-element.30), channel_id=1, source_target_pairs={{0,8},{1,5},{2,10},{3,7},{4,12},{9,13},{6,14},{11,15},{8,0},{5,1},... | collective-permute-start | bytes 208904 | tf_op jit(solution)/shard_map/ppermute | solution.py:381
  22.4 5.4 %collective-permute-start.1 = (f32[136,128]{1,0:T(8,128)S(1)}, f32[136,128]{1,0:T(8,128)S(1)}, u32[]{:S(2)}, u32[]{:S(2)}) collective-permute-start(f32[136,128]{1,0:T(8,128)S(1)} %get-tuple-element.29), channel_id=1, source_target_pairs={{0,16},{1,17},{2,18},{3,19},{4,20},{9,25},{6,22},{11,27},{8,24},{5... | collective-permute-start | bytes 208904 | tf_op jit(solution)/shard_map/ppermute | solution.py:381
  25.1 15.0 %collective-permute-start.11 = (f32[512,128]{1,0:T(8,128)S(1)}, f32[512,128]{1,0:T(8,128)S(1)}, u32[]{:S(2)}, u32[]{:S(2)}) collective-permute-start(f32[512,128]{1,0:T(8,128)S(1)} %get-tuple-element.37), channel_id=1, source_target_pairs={{0,1},{1,2},{2,3},{3,0},{4,5},{5,6},{6,7},{7,4},{8,9},{9,10},{10,1... | collective-permute-start | bytes 786440 | tf_op jit(solution)/shard_map/ppermute | solution.py:367
  27.9 5.8 %collective-permute-start.5 = (f32[136,128]{1,0:T(8,128)S(1)}, f32[136,128]{1,0:T(8,128)S(1)}, u32[]{:S(2)}, u32[]{:S(2)}) collective-permute-start(f32[136,128]{1,0:T(8,128)S(1)} %multiply_select_fusion.refs_0_), channel_id=1, source_target_pairs={{0,8},{1,5},{2,10},{3,7},{4,12},{9,13},{6,14},{11,15},{8,0},{5,1},... | collective-permute-start | bytes 208904 | tf_op jit(solution)/shard_map/ppermute | solution.py:381
  29.8 7.7 %collective-permute-start.7 = (f32[136,128]{1,0:T(8,128)S(1)}, f32[136,128]{1,0:T(8,128)S(1)}, u32[]{:S(2)}, u32[]{:S(2)}) collective-permute-start(f32[136,128]{1,0:T(8,128)S(1)} %multiply_select_fusion.refs_0_), channel_id=1, source_target_pairs={{0,16},{1,17},{2,18},{3,19},{4,20},{9,25},{6,22},{11,27},{8,24},{5... | collective-permute-start | bytes 208904 | tf_op jit(solution)/shard_map/ppermute | solution.py:381
  32.2 6.8 %collective-permute-start.9 = (f32[136,128]{1,0:T(8,128)S(1)}, f32[136,128]{1,0:T(8,128)S(1)}, u32[]{:S(2)}, u32[]{:S(2)}) collective-permute-start(f32[136,128]{1,0:T(8,128)S(1)} %multiply_select_fusion.refs_0_), channel_id=1, source_target_pairs={{0,24},{1,21},{2,26},{3,23},{4,28},{9,29},{6,30},{11,31},{8,16},{5... | collective-permute-start | bytes 208904 | tf_op jit(solution)/shard_map/ppermute | solution.py:381
  32.4 8.5 %collective-permute-start.4 = (f32[136,128]{1,0:T(8,128)S(1)}, f32[136,128]{1,0:T(8,128)S(1)}, u32[]{:S(2)}, u32[]{:S(2)}) collective-permute-start(f32[136,128]{1,0:T(8,128)S(1)} %multiply_select_fusion.refs_0_), channel_id=1, source_target_pairs={{0,4},{1,9},{2,6},{3,11},{4,0},{9,1},{6,2},{11,3},{8,12},{5,13},{1... | collective-permute-start | bytes 208904 | tf_op jit(solution)/shard_map/ppermute | solution.py:381
  33.7 7.1 %collective-permute-start.6 = (f32[136,128]{1,0:T(8,128)S(1)}, f32[136,128]{1,0:T(8,128)S(1)}, u32[]{:S(2)}, u32[]{:S(2)}) collective-permute-start(f32[136,128]{1,0:T(8,128)S(1)} %collective-permute-done.5.refs_2_), channel_id=1, source_target_pairs={{0,4},{1,9},{2,6},{3,11},{4,0},{9,1},{6,2},{11,3},{8,12},{5,13},{1... | collective-permute-start | bytes 208904 | tf_op jit(solution)/shard_map/ppermute | solution.py:381
  37.5 4.3 %collective-permute-start.8 = (f32[136,128]{1,0:T(8,128)S(1)}, f32[136,128]{1,0:T(8,128)S(1)}, u32[]{:S(2)}, u32[]{:S(2)}) collective-permute-start(f32[136,128]{1,0:T(8,128)S(1)} %collective-permute-done.7.refs_4_), channel_id=1, source_target_pairs={{0,4},{1,9},{2,6},{3,11},{4,0},{9,1},{6,2},{11,3},{8,12},{5,13},{1... | collective-permute-start | bytes 208904 | tf_op jit(solution)/shard_map/ppermute | solution.py:381
  39.1 4.3 %collective-permute-start.10 = (f32[136,128]{1,0:T(8,128)S(1)}, f32[136,128]{1,0:T(8,128)S(1)}, u32[]{:S(2)}, u32[]{:S(2)}) collective-permute-start(f32[136,128]{1,0:T(8,128)S(1)} %collective-permute-done.9.refs_6_), channel_id=1, source_target_pairs={{0,4},{1,9},{2,6},{3,11},{4,0},{9,1},{6,2},{11,3},{8,12},{5,13},{1... | collective-permute-start | bytes 208904 | tf_op jit(solution)/shard_map/ppermute | solution.py:381
where the time goes:
time: 44.4 us; the launch traced here: 44.3 us
  starting transfers between devices  17.3 us (39%)
  Pallas kernels  13.3 us (30%)
  waiting for transfers between devices  12 us (27%)
  other arithmetic  0.91 us (2%)
  between operations  0.72 us (2%)
    ppermute x11, starting transfers between devices, moved(): return lax.ppermute(value, ('ep', 'corner'), pairs)  14.1 us
    ppermute x11, waiting for transfers between devices, moved(): return lax.ppermute(value, ('ep', 'corner'), pairs)  12 us
    pallas_call x2, Pallas kernels, run_hist(): pl.pallas_call(functools.partial(hist_kernel, C, KT, n), in_specs=[smem]...  11 us
    ppermute x3, starting transfers between devices, rotate(): lax.ppermute(value, axis, [(i, (i + distance) % size) for i in range(size)])  3.13 us
    pallas_call x1, Pallas kernels, run_prep(): pl.pallas_call(functools.partial(prep_kernel, C), in_specs=[pl.BlockSpec(...  1.46 us
  transfers between devices with their start and end apart: 14, of which 8 were waited for; matrix products, arithmetic and copies ran while one was open for 2% of the time, Pallas kernels for 25%

commit v1 on v0

--- a/solution.py
+++ b/solution.py
@@ -312,11 +312,9 @@
     )(place, coarse, fine, slack, *prior)
 
 
-def final_kernel(C, own, share, scale, me_ref, *refs):
-    n = len(refs) - 5
-    pieces = refs[:n]
-    hist_ref, part_ref, share_ref, tns_ref, wns_ref = refs[n:]
-    half = C // 2
+def final_kernel(own, me_ref, *refs):
+    pieces, hist_ref = refs[:-1], refs[-1]
+    n = len(pieces)
     each = hist_ref.shape[0] // GROUPS // 2
     for d in range(n):
         source = me_ref[0] ^ d
@@ -324,11 +322,16 @@
         for p in range(own):
             at = pl.multiple_of((place * own + p) * 2 * each + side * each, 8)
             hist_ref[pl.ds(at, each), :] = pieces[d][p * each:(p + 1) * each, :]
+
+
+def small_kernel(C, share, scale, me_ref, mine_ref, other_ref, part_ref, share_ref, tns_ref, wns_ref):
+    half = C // 2
+    top = mine_ref.shape[0] - EXTRA
     tns = jnp.zeros((C, 2), jnp.float32)
     wns = jnp.zeros((C, 2), jnp.float32)
     row = lax.broadcasted_iota(jnp.int32, (C, 2), 0)
     col = lax.broadcasted_iota(jnp.int32, (C, 2), 1)
-    mine, other = pieces[0][own * each:, :], pieces[1][own * each:, :]
+    mine, other = mine_ref[top:top + EXTRA, :], other_ref[top:top + EXTRA, :]
     even = me_ref[0] % 2 == 0
     for side in range(2):
         tile = jnp.where(even, mine, other) if side == 0 else jnp.where(even, other, mine)
@@ -345,21 +348,31 @@
     wns_ref[...] = wns
 
 
-def run_final(me, pieces, C, own, rows, endpoints):
+def run_final(me, pieces, own, rows):
     vm = pl.BlockSpec(memory_space=pltpu.VMEM)
     return pl.pallas_call(
-        functools.partial(final_kernel, C, own, GROUPS / endpoints, 1.0 / endpoints),
+        functools.partial(final_kernel, own),
         in_specs=[pl.BlockSpec(memory_space=pltpu.SMEM)] + [vm] * len(pieces),
+        out_shape=jax.ShapeDtypeStruct((GROUPS * rows, LANES), jnp.float32),
+        compiler_params=pltpu.CompilerParams(vmem_limit_bytes=VMEM),
+        name="final",
+    )(me, *pieces)
+
+
+def run_small(me, mine, other, C, endpoints):
+    vm = pl.BlockSpec(memory_space=pltpu.VMEM)
+    return pl.pallas_call(
+        functools.partial(small_kernel, C, GROUPS / endpoints, 1.0 / endpoints),
+        in_specs=[pl.BlockSpec(memory_space=pltpu.SMEM), vm, vm],
         out_shape=[
-            jax.ShapeDtypeStruct((GROUPS * rows, LANES), jnp.float32),
             jax.ShapeDtypeStruct((C, 2, GROUPS), jnp.float32),
             jax.ShapeDtypeStruct((1, GROUPS), jnp.float32),
             jax.ShapeDtypeStruct((C, 2), jnp.float32),
             jax.ShapeDtypeStruct((C, 2), jnp.float32),
         ],
         compiler_params=pltpu.CompilerParams(vmem_limit_bytes=VMEM),
-        name="final",
-    )(me, *pieces)
+        name="small",
+    )(me, mine, other)
 
 
 def rotate(value, axis, distance):
@@ -425,10 +438,11 @@
     pieces[1] = moved(mine, lambda i: i ^ 1)
     for d in range(1, rest):
         pieces[2 * d + 1] = moved(pieces[2 * d], lambda i: i ^ 1)
+    part_tns, part_share, tns, wns = run_small(me.reshape(1), mine, pieces[1], C, endpoints)
     worst = functools.reduce(jnp.minimum, shares, near)
     worst = worst.reshape(lines, 2, LANES)
     worst = worst.transpose(1, 0, 2).reshape(2, rows)
-    full, part_tns, part_share, tns, wns = run_final(me.reshape(1), pieces, C, own, 2 * each, endpoints)
+    full = run_final(me.reshape(1), pieces, own, 2 * each)
     part_hist = full.reshape(GROUPS, C, nblk, 2, LANES).transpose(0, 1, 3, 2, 4).reshape(GROUPS, C, 2, bins)
     part_tns = part_tns.transpose(2, 0, 1)
     part_share = part_share.reshape(GROUPS)

time: 44.4 us -> 44.4 us (level)
  Pallas kernels: 13.3 us -> 14 us
  waiting for transfers between devices: 12 us -> 11.4 us
    ppermute x11, waiting for transfers between devices: 12 us -> 11.3 us  [moved(): return lax.ppermute(value, ('ep', 'corner'), pairs)]
    pallas_call x1 -> x2, Pallas kernels: 0.85 us -> 1.53 us  [the longest x1 0.83 us: run_final(): pl.pallas_call(functools.partial(final_kernel, own), in_specs=[pl.BlockSp...]
  transfers between devices with their start and end apart: 14 -> 14, of which waited for: 8 -> 8; matrix products, arithmetic and copies ran while one was open for 2% -> 2% of each run, Pallas kernels for 25% -> 27%
where the time goes in v1:
time: 44.4 us; the launch traced here: 44.2 us
  starting transfers between devices  17.3 us (39%)
  Pallas kernels  14 us (32%)
  waiting for transfers between devices  11.4 us (26%)
  other arithmetic  0.91 us (2%)
  between operations  0.72 us (2%)
    ppermute x11, starting transfers between devices, moved(): return lax.ppermute(value, ('ep', 'corner'), pairs)  14.1 us
    ppermute x11, waiting for transfers between devices, moved(): return lax.ppermute(value, ('ep', 'corner'), pairs)  11.3 us
    pallas_call x2, Pallas kernels, run_hist(): pl.pallas_call(functools.partial(hist_kernel, C, KT, n), in_specs=[smem]...  11 us
    ppermute x3, starting transfers between devices, rotate(): lax.ppermute(value, axis, [(i, (i + distance) % size) for i in range(size)])  3.13 us
    pallas_call x1, Pallas kernels, run_prep(): pl.pallas_call(functools.partial(prep_kernel, C), in_specs=[pl.BlockSpec(...  1.46 us
  transfers between devices with their start and end apart: 14, of which 8 were waited for; matrix products, arithmetic and copies ran while one was open for 2% of the time, Pallas kernels for 27%

profile of v1, /device:TPU:0, one launch (start us, length us, event | category | flops | bytes accessed | tf_op | source)
XLA Modules:
  0.0 44.2 jit_solution(14669978813985340286)
XLA Ops:
  0.7 1.5 %prep.1 = (s32[4,128]{1,0:T(4,128)S(1)}, s32[4,128]{1,0:T(4,128)S(1)}, f32[512,128]{1,0:T(8,128)S(1)}, f32[3,256,128]{2,1,0:T(8,128)S(1)}, f32[3,256,128]{2,1,0:T(8,128)S(1)}) custom-call(s32[1]{0:T(128)} %bitcast.2.side_ref, s32[4,128]{1,0:T(4,128)} %bitcast.44, s32[256,128]{1,0:T(8,128)} %bitcast.43, f32[512,128]{1,0:T(8,128)} %bitcast.39, ...), custom_call_target="tpu_custom_call" | custom-call | tf_op jit(solution)/shard_map/prep/pallas_call | solution.py:116
  2.1 2.5 %collective-permute-start.13 = (f32[512,128]{1,0:T(8,128)S(1)}, f32[512,128]{1,0:T(8,128)S(1)}, u32[]{:S(2)}, u32[]{:S(2)}) collective-permute-start(f32[512,128]{1,0:T(8,128)S(1)} %get-tuple-element.35), channel_id=1, source_target_pairs={{0,3},{1,0},{2,1},{3,2},{4,7},{5,4},{6,5},{7,6},{8,11},{9,8},{10,9... | collective-permute-start | bytes 786440 | tf_op jit(solution)/shard_map/ppermute | solution.py:380
  4.6 0.6 %collective-permute-start.12 = (f32[512,128]{1,0:T(8,128)S(1)}, f32[512,128]{1,0:T(8,128)S(1)}, u32[]{:S(2)}, u32[]{:S(2)}) collective-permute-start(f32[512,128]{1,0:T(8,128)S(1)} %get-tuple-element.35), channel_id=1, source_target_pairs={{0,2},{1,3},{2,0},{3,1},{4,6},{5,7},{6,4},{7,5},{8,10},{9,11},{10,... | collective-permute-start | bytes 786440 | tf_op jit(solution)/shard_map/ppermute | solution.py:380
  5.3 1.5 %collective-permute-start = (f32[3,256,128]{2,1,0:T(8,128)S(1)}, f32[3,256,128]{2,1,0:T(8,128)S(1)}, u32[]{:S(2)}, u32[]{:S(2)}) collective-permute-start(f32[3,256,128]{2,1,0:T(8,128)S(1)} %get-tuple-element.23), channel_id=1, source_target_pairs={{0,4},{1,9},{2,6},{3,11},{4,0},{9,1},{6,2},{11,3},{8,12},{5,13},{1... | collective-permute-start | bytes 1179656 | tf_op jit(solution)/shard_map/ppermute | solution.py:394
  6.8 5.4 %hist.2 = (f32[2,144,256]{2,1,0:T(8,128)S(1)}, f32[2,8,128]{2,1,0:T(8,128)S(1)}) custom-call(s32[1]{0:T(128)} %bitcast.1.place_ref, s32[4,128]{1,0:T(4,128)S(1)} %get-tuple-element.21.coarse_ref, s32[4,128]{1,0:T(4,128)S(1)} %get-tuple-element.22.fine_ref, f32[3,256,128]{2,1,0:T(8,128)S(1)} %get-tuple-element.24.slack_ref), custom_call_target="tpu_custom_call" | custom-call | flops 4831838208 | bytes 786432 | tf_op jit(solution)/shard_map/hist/pallas_call | solution.py:302
  12.2 0.9 %collective-permute-done.slack_ref = f32[3,256,128]{2,1,0:T(8,128)S(1)} collective-permute-done((f32[3,256,128]{2,1,0:T(8,128)S(1)}, f32[3,256,128]{2,1,0:T(8,128)S(1)}, u32[]{:S(2)}, u32[]{:S(2)}) %collective-permute-start) | collective-permute-done | bytes 393248 | tf_op jit(solution)/shard_map/ppermute | solution.py:394
  13.0 5.6 %hist.3 = (f32[136,128]{1,0:T(8,128)S(1)}, f32[136,128]{1,0:T(8,128)S(1)}, f32[136,128]{1,0:T(8,128)S(1)}, f32[136,128]{1,0:T(8,128)S(1)}, f32[2,8,128]{2,1,0:T(8,128)}) custom-call(s32[1]{0:T(128)} %bitcast.1.place_ref, s32[4,128]{1,0:T(4,128)S(1)} %get-tuple-element.21.coarse_ref, s32[4,128]{1,0:T(4,128)S(1)} %get-tuple-element.22.fine_ref, ...), custom_call_target="tpu_custom_call" | custom-call | flops 4831838208 | bytes 786432 | tf_op jit(solution)/shard_map/hist/pallas_call | solution.py:302
  18.7 3.7 %collective-permute-start.3 = (f32[136,128]{1,0:T(8,128)S(1)}, f32[136,128]{1,0:T(8,128)S(1)}, u32[]{:S(2)}, u32[]{:S(2)}) collective-permute-start(f32[136,128]{1,0:T(8,128)S(1)} %get-tuple-element.30), channel_id=1, source_target_pairs={{0,24},{1,21},{2,26},{3,23},{4,28},{9,29},{6,30},{11,31},{8,16},{5... | collective-permute-start | bytes 208904 | tf_op jit(solution)/shard_map/ppermute | solution.py:394
  22.3 0.0 collective-permute-start.2
  22.4 0.8 %collective-permute-start.1 = (f32[136,128]{1,0:T(8,128)S(1)}, f32[136,128]{1,0:T(8,128)S(1)}, u32[]{:S(2)}, u32[]{:S(2)}) collective-permute-start(f32[136,128]{1,0:T(8,128)S(1)} %get-tuple-element.28), channel_id=1, source_target_pairs={{0,16},{1,17},{2,18},{3,19},{4,20},{9,25},{6,22},{11,27},{8,24},{5... | collective-permute-start | bytes 208904 | tf_op jit(solution)/shard_map/ppermute | solution.py:394
  23.1 1.9 %collective-permute-done.3 = f32[136,128]{1,0:T(8,128)S(1)} collective-permute-done((f32[136,128]{1,0:T(8,128)S(1)}, f32[136,128]{1,0:T(8,128)S(1)}, u32[]{:S(2)}, u32[]{:S(2)}) %collective-permute-start.3) | collective-permute-done | bytes 69664 | tf_op jit(solution)/shard_map/ppermute | solution.py:394
  25.1 0.0 collective-permute-start.11
  25.1 1.7 %collective-permute-done.2 = f32[136,128]{1,0:T(8,128)S(1)} collective-permute-done((f32[136,128]{1,0:T(8,128)S(1)}, f32[136,128]{1,0:T(8,128)S(1)}, u32[]{:S(2)}, u32[]{:S(2)}) %collective-permute-start.2) | collective-permute-done | bytes 69664 | tf_op jit(solution)/shard_map/ppermute | solution.py:394
  26.8 1.0 %collective-permute-done.1 = f32[136,128]{1,0:T(8,128)S(1)} collective-permute-done((f32[136,128]{1,0:T(8,128)S(1)}, f32[136,128]{1,0:T(8,128)S(1)}, u32[]{:S(2)}, u32[]{:S(2)}) %collective-permute-start.1) | collective-permute-done | bytes 69664 | tf_op jit(solution)/shard_map/ppermute | solution.py:394
  27.8 0.1 multiply_select_fusion.refs_0_.mine_ref
  27.9 1.8 %collective-permute-start.5 = (f32[136,128]{1,0:T(8,128)S(1)}, f32[136,128]{1,0:T(8,128)S(1)}, u32[]{:S(2)}, u32[]{:S(2)}) collective-permute-start(f32[136,128]{1,0:T(8,128)S(1)} %multiply_select_fusion.refs_0_.mine_ref), channel_id=1, source_target_pairs={{0,8},{1,5},{2,10},{3,7},{4,12},{9,13},{6,14},{11,15},{8,0},{5,1},... | collective-permute-start | bytes 208904 | tf_op jit(solution)/shard_map/ppermute | solution.py:394
  29.8 2.5 %collective-permute-start.7 = (f32[136,128]{1,0:T(8,128)S(1)}, f32[136,128]{1,0:T(8,128)S(1)}, u32[]{:S(2)}, u32[]{:S(2)}) collective-permute-start(f32[136,128]{1,0:T(8,128)S(1)} %multiply_select_fusion.refs_0_.mine_ref), channel_id=1, source_target_pairs={{0,16},{1,17},{2,18},{3,19},{4,20},{9,25},{6,22},{11,27},{8,24},{5... | collective-permute-start | bytes 208904 | tf_op jit(solution)/shard_map/ppermute | solution.py:394
  32.2 0.0 collective-permute-done.13
  32.3 0.1 collective-permute-start.9
  32.4 0.0 collective-permute-done.12
  32.4 1.3 %collective-permute-start.4 = (f32[136,128]{1,0:T(8,128)S(1)}, f32[136,128]{1,0:T(8,128)S(1)}, u32[]{:S(2)}, u32[]{:S(2)}) collective-permute-start(f32[136,128]{1,0:T(8,128)S(1)} %multiply_select_fusion.refs_0_.mine_ref), channel_id=1, source_target_pairs={{0,4},{1,9},{2,6},{3,11},{4,0},{9,1},{6,2},{11,3},{8,12},{5,13},{1... | collective-permute-start | bytes 208904 | tf_op jit(solution)/shard_map/ppermute | solution.py:394
  33.7 0.0 collective-permute-done.5.refs_2_
  33.7 0.7 %collective-permute-start.6 = (f32[136,128]{1,0:T(8,128)S(1)}, f32[136,128]{1,0:T(8,128)S(1)}, u32[]{:S(2)}, u32[]{:S(2)}) collective-permute-start(f32[136,128]{1,0:T(8,128)S(1)} %collective-permute-done.5.refs_2_), channel_id=1, source_target_pairs={{0,4},{1,9},{2,6},{3,11},{4,0},{9,1},{6,2},{11,3},{8,12},{5,13},{1... | collective-permute-start | bytes 208904 | tf_op jit(solution)/shard_map/ppermute | solution.py:394
  34.4 3.1 %collective-permute-done.7.refs_4_ = f32[136,128]{1,0:T(8,128)S(1)} collective-permute-done((f32[136,128]{1,0:T(8,128)S(1)}, f32[136,128]{1,0:T(8,128)S(1)}, u32[]{:S(2)}, u32[]{:S(2)}) %collective-permute-start.7) | collective-permute-done | bytes 69664 | tf_op jit(solution)/shard_map/ppermute | solution.py:394
  37.5 0.8 %collective-permute-start.8 = (f32[136,128]{1,0:T(8,128)S(1)}, f32[136,128]{1,0:T(8,128)S(1)}, u32[]{:S(2)}, u32[]{:S(2)}) collective-permute-start(f32[136,128]{1,0:T(8,128)S(1)} %collective-permute-done.7.refs_4_), channel_id=1, source_target_pairs={{0,4},{1,9},{2,6},{3,11},{4,0},{9,1},{6,2},{11,3},{8,12},{5,13},{1... | collective-permute-start | bytes 208904 | tf_op jit(solution)/shard_map/ppermute | solution.py:394
  38.2 0.9 %collective-permute-done.9.refs_6_ = f32[136,128]{1,0:T(8,128)S(1)} collective-permute-done((f32[136,128]{1,0:T(8,128)S(1)}, f32[136,128]{1,0:T(8,128)S(1)}, u32[]{:S(2)}, u32[]{:S(2)}) %collective-permute-start.9) | collective-permute-done | bytes 69664 | tf_op jit(solution)/shard_map/ppermute | solution.py:394
  39.1 0.9 %collective-permute-start.10 = (f32[136,128]{1,0:T(8,128)S(1)}, f32[136,128]{1,0:T(8,128)S(1)}, u32[]{:S(2)}, u32[]{:S(2)}) collective-permute-start(f32[136,128]{1,0:T(8,128)S(1)} %collective-permute-done.9.refs_6_), channel_id=1, source_target_pairs={{0,4},{1,9},{2,6},{3,11},{4,0},{9,1},{6,2},{11,3},{8,12},{5,13},{1... | collective-permute-start | bytes 208904 | tf_op jit(solution)/shard_map/ppermute | solution.py:394
  40.0 0.0 collective-permute-done.11
  40.0 0.8 %minimum_minimum_fusion = f32[512,128]{1,0:T(8,128)} fusion(f32[512,128]{1,0:T(8,128)S(1)} %collective-permute-done.13, f32[512,128]{1,0:T(8,128)S(1)} %collective-permute-done.12, f32[512,128]{1,0:T(8,128)S(1)} %get-tuple-element.35, f32[512,128]{1,0:T(8,128)S(1)} %collective-permute-done.11), kind=kLoop, calls=%fused_computation | loop fusion | flops 196608 | bytes 1310720 | tf_op jit(solution)/shard_map/min | solution.py:442
  40.8 0.0 collective-permute-done.4.refs_1_.other_ref
  40.8 0.7 %small.1 = (f32[2,2,64]{2,1,0:T(2,128)}, f32[1,64]{1,0:T(1,128)}, f32[2,2]{1,0:T(2,128)}, f32[2,2]{1,0:T(2,128)}) custom-call(s32[1]{0:T(128)} %bitcast.me_ref, f32[136,128]{1,0:T(8,128)S(1)} %multiply_select_fusion.refs_0_.mine_ref, f32[136,128]{1,0:T(8,128)S(1)} %collective-permute-done.4.refs_1_.other_ref), custom_call_target="tpu_custom_call" | custom-call | tf_op jit(solution)/shard_map/small/pallas_call | solution.py:364
  41.5 0.0 collective-permute-done.6.refs_3_
  41.5 0.2 collective-permute-done.8.refs_5_
  41.8 1.6 %collective-permute-done.10.refs_7_ = f32[136,128]{1,0:T(8,128)S(1)} collective-permute-done((f32[136,128]{1,0:T(8,128)S(1)}, f32[136,128]{1,0:T(8,128)S(1)}, u32[]{:S(2)}, u32[]{:S(2)}) %collective-permute-start.10) | collective-permute-done | bytes 69664 | tf_op jit(solution)/shard_map/ppermute | solution.py:394
  43.4 0.8 %final.1 = f32[1024,128]{1,0:T(8,128)} custom-call(s32[1]{0:T(128)} %bitcast.me_ref, f32[136,128]{1,0:T(8,128)S(1)} %multiply_select_fusion.refs_0_.mine_ref, f32[136,128]{1,0:T(8,128)S(1)} %collective-permute-done.4.refs_1_.other_ref, f32[136,128]{1,0:T(8,128)S(1)} %collective-permute-done.5.refs_2_, f32[136,128]{1,0:T(8,128)S(1)} %collective-permute-done.6.refs_3_, ...), custom_call_target="tpu_custom_call" | custom-call | tf_op jit(solution)/shard_map/final/pallas_call | solution.py:353
  (2 shorter events, 0.0 us)
Async XLA Ops:
  2.1 30.1 %collective-permute-start.13 = (f32[512,128]{1,0:T(8,128)S(1)}, f32[512,128]{1,0:T(8,128)S(1)}, u32[]{:S(2)}, u32[]{:S(2)}) collective-permute-start(f32[512,128]{1,0:T(8,128)S(1)} %get-tuple-element.35), channel_id=1, source_target_pairs={{0,3},{1,0},{2,1},{3,2},{4,7},{5,4},{6,5},{7,6},{8,11},{9,8},{10,9... | collective-permute-start | bytes 786440 | tf_op jit(solution)/shard_map/ppermute | solution.py:380
  4.6 27.7 %collective-permute-start.12 = (f32[512,128]{1,0:T(8,128)S(1)}, f32[512,128]{1,0:T(8,128)S(1)}, u32[]{:S(2)}, u32[]{:S(2)}) collective-permute-start(f32[512,128]{1,0:T(8,128)S(1)} %get-tuple-element.35), channel_id=1, source_target_pairs={{0,2},{1,3},{2,0},{3,1},{4,6},{5,7},{6,4},{7,5},{8,10},{9,11},{10,... | collective-permute-start | bytes 786440 | tf_op jit(solution)/shard_map/ppermute | solution.py:380
  5.3 7.8 %collective-permute-start = (f32[3,256,128]{2,1,0:T(8,128)S(1)}, f32[3,256,128]{2,1,0:T(8,128)S(1)}, u32[]{:S(2)}, u32[]{:S(2)}) collective-permute-start(f32[3,256,128]{2,1,0:T(8,128)S(1)} %get-tuple-element.23), channel_id=1, source_target_pairs={{0,4},{1,9},{2,6},{3,11},{4,0},{9,1},{6,2},{11,3},{8,12},{5,13},{1... | collective-permute-start | bytes 1179656 | tf_op jit(solution)/shard_map/ppermute | solution.py:394
  18.7 6.4 %collective-permute-start.3 = (f32[136,128]{1,0:T(8,128)S(1)}, f32[136,128]{1,0:T(8,128)S(1)}, u32[]{:S(2)}, u32[]{:S(2)}) collective-permute-start(f32[136,128]{1,0:T(8,128)S(1)} %get-tuple-element.30), channel_id=1, source_target_pairs={{0,24},{1,21},{2,26},{3,23},{4,28},{9,29},{6,30},{11,31},{8,16},{5... | collective-permute-start | bytes 208904 | tf_op jit(solution)/shard_map/ppermute | solution.py:394
  22.3 4.5 %collective-permute-start.2 = (f32[136,128]{1,0:T(8,128)S(1)}, f32[136,128]{1,0:T(8,128)S(1)}, u32[]{:S(2)}, u32[]{:S(2)}) collective-permute-start(f32[136,128]{1,0:T(8,128)S(1)} %get-tuple-element.29), channel_id=1, source_target_pairs={{0,8},{1,5},{2,10},{3,7},{4,12},{9,13},{6,14},{11,15},{8,0},{5,1},... | collective-permute-start | bytes 208904 | tf_op jit(solution)/shard_map/ppermute | solution.py:394
  22.4 5.4 %collective-permute-start.1 = (f32[136,128]{1,0:T(8,128)S(1)}, f32[136,128]{1,0:T(8,128)S(1)}, u32[]{:S(2)}, u32[]{:S(2)}) collective-permute-start(f32[136,128]{1,0:T(8,128)S(1)} %get-tuple-element.28), channel_id=1, source_target_pairs={{0,16},{1,17},{2,18},{3,19},{4,20},{9,25},{6,22},{11,27},{8,24},{5... | collective-permute-start | bytes 208904 | tf_op jit(solution)/shard_map/ppermute | solution.py:394
  25.1 15.0 %collective-permute-start.11 = (f32[512,128]{1,0:T(8,128)S(1)}, f32[512,128]{1,0:T(8,128)S(1)}, u32[]{:S(2)}, u32[]{:S(2)}) collective-permute-start(f32[512,128]{1,0:T(8,128)S(1)} %get-tuple-element.35), channel_id=1, source_target_pairs={{0,1},{1,2},{2,3},{3,0},{4,5},{5,6},{6,7},{7,4},{8,9},{9,10},{10,1... | collective-permute-start | bytes 786440 | tf_op jit(solution)/shard_map/ppermute | solution.py:380
  27.9 5.8 %collective-permute-start.5 = (f32[136,128]{1,0:T(8,128)S(1)}, f32[136,128]{1,0:T(8,128)S(1)}, u32[]{:S(2)}, u32[]{:S(2)}) collective-permute-start(f32[136,128]{1,0:T(8,128)S(1)} %multiply_select_fusion.refs_0_.mine_ref), channel_id=1, source_target_pairs={{0,8},{1,5},{2,10},{3,7},{4,12},{9,13},{6,14},{11,15},{8,0},{5,1},... | collective-permute-start | bytes 208904 | tf_op jit(solution)/shard_map/ppermute | solution.py:394
  29.8 7.7 %collective-permute-start.7 = (f32[136,128]{1,0:T(8,128)S(1)}, f32[136,128]{1,0:T(8,128)S(1)}, u32[]{:S(2)}, u32[]{:S(2)}) collective-permute-start(f32[136,128]{1,0:T(8,128)S(1)} %multiply_select_fusion.refs_0_.mine_ref), channel_id=1, source_target_pairs={{0,16},{1,17},{2,18},{3,19},{4,20},{9,25},{6,22},{11,27},{8,24},{5... | collective-permute-start | bytes 208904 | tf_op jit(solution)/shard_map/ppermute | solution.py:394
  32.3 6.8 %collective-permute-start.9 = (f32[136,128]{1,0:T(8,128)S(1)}, f32[136,128]{1,0:T(8,128)S(1)}, u32[]{:S(2)}, u32[]{:S(2)}) collective-permute-start(f32[136,128]{1,0:T(8,128)S(1)} %multiply_select_fusion.refs_0_.mine_ref), channel_id=1, source_target_pairs={{0,24},{1,21},{2,26},{3,23},{4,28},{9,29},{6,30},{11,31},{8,16},{5... | collective-permute-start | bytes 208904 | tf_op jit(solution)/shard_map/ppermute | solution.py:394
  32.4 8.5 %collective-permute-start.4 = (f32[136,128]{1,0:T(8,128)S(1)}, f32[136,128]{1,0:T(8,128)S(1)}, u32[]{:S(2)}, u32[]{:S(2)}) collective-permute-start(f32[136,128]{1,0:T(8,128)S(1)} %multiply_select_fusion.refs_0_.mine_ref), channel_id=1, source_target_pairs={{0,4},{1,9},{2,6},{3,11},{4,0},{9,1},{6,2},{11,3},{8,12},{5,13},{1... | collective-permute-start | bytes 208904 | tf_op jit(solution)/shard_map/ppermute | solution.py:394
  33.7 7.8 %collective-permute-start.6 = (f32[136,128]{1,0:T(8,128)S(1)}, f32[136,128]{1,0:T(8,128)S(1)}, u32[]{:S(2)}, u32[]{:S(2)}) collective-permute-start(f32[136,128]{1,0:T(8,128)S(1)} %collective-permute-done.5.refs_2_), channel_id=1, source_target_pairs={{0,4},{1,9},{2,6},{3,11},{4,0},{9,1},{6,2},{11,3},{8,12},{5,13},{1... | collective-permute-start | bytes 208904 | tf_op jit(solution)/shard_map/ppermute | solution.py:394
  37.5 4.3 %collective-permute-start.8 = (f32[136,128]{1,0:T(8,128)S(1)}, f32[136,128]{1,0:T(8,128)S(1)}, u32[]{:S(2)}, u32[]{:S(2)}) collective-permute-start(f32[136,128]{1,0:T(8,128)S(1)} %collective-permute-done.7.refs_4_), channel_id=1, source_target_pairs={{0,4},{1,9},{2,6},{3,11},{4,0},{9,1},{6,2},{11,3},{8,12},{5,13},{1... | collective-permute-start | bytes 208904 | tf_op jit(solution)/shard_map/ppermute | solution.py:394
  39.1 4.3 %collective-permute-start.10 = (f32[136,128]{1,0:T(8,128)S(1)}, f32[136,128]{1,0:T(8,128)S(1)}, u32[]{:S(2)}, u32[]{:S(2)}) collective-permute-start(f32[136,128]{1,0:T(8,128)S(1)} %collective-permute-done.9.refs_6_), channel_id=1, source_target_pairs={{0,4},{1,9},{2,6},{3,11},{4,0},{9,1},{6,2},{11,3},{8,12},{5,13},{1... | collective-permute-start | bytes 208904 | tf_op jit(solution)/shard_map/ppermute | solution.py:394
